TPU v7x, 32 devices: a whole 2x2x4 slice. The times are simulated.
32 devices in a mesh: gx: 4 (over x, core), gy: 8 (over z, y).
Axes of the slice: x: 2, y: 2, z: 4, core: 2. Of those that a mesh axis runs over, the one named last changes fastest.
Arguments:
- normal_matrix: float32 [4096, 4096], P(('gx', 'gy')), may hold values from -1 to 4, as said below
- right_sides: float32 [4096, 32], P(('gx', 'gy')), may hold values from -6 to 6
- tile_order: int32 [32], replicated, may hold values from 0 to 31, as said below
- inner_order: int32 [32, 128], replicated, may hold values from 0 to 127, each once within a row
- block_lengths: int32 [16], replicated, may hold values from 1 to 3, as said below
Outputs:
- renumbered: float32 [4096, 4096], P(None, ('gx', 'gy'))
- solution: float32 [4096, 32], P(('gx', 'gy'))
Inputs may be any that keep to these rules, and one draw needn't show every extreme that they name: `normal_matrix`: symmetric positive definite. `tile_order`: a permutation. `inner_order`: each row a permutation. `block_lengths`: the lengths sum to 32, and the largest is 3.
All inputs are finite; a program needn't handle non-finite values.
Results may differ from a plain program's by a relative error of at most 0.0003.
Values sent between devices are 32-bit elements; how exact they have to be, the bound alone decides.
No kernel may reach another device: no remote copies, remote signals or barrier semaphores. Data moves between devices by JAX's collectives and lax.ppermute only.
A program may use at most 128 MiB of HBM per device.

v0:
```python
import jax
import jax.numpy as jnp
from jax import lax
from jax.sharding import PartitionSpec as P

MOSTT = 3


def from_behind(value, axis, steps):
    count = lax.axis_size(axis)
    leading, last = (max(0, -steps), min(count, count - steps))
    return lax.ppermute(value, axis, [(source, source + steps) for source in range(leading, last)])


def fetch_columns(window_piece, offset):
    return from_behind(window_piece, ("gx", "gy"), -offset)


def fetch_residual(residual, offset):
    return from_behind(residual, ("gx", "gy"), -offset)


def return_solution(solved_rows, offset):
    return from_behind(solved_rows, ("gx", "gy"), offset)


def body(normal_matrix, right_sides, tile_order, inner_order, block_lengths):
    tile_width = normal_matrix.shape[0]
    count_gx = lax.axis_size("gx")
    count_gy = lax.axis_size("gy")
    tile_count = count_gx * count_gy
    self_index = lax.axis_index(("gx", "gy"))
    new_to_old = (tile_order[:, None] * tile_width + inner_order).reshape(-1)
    row_slab = jnp.take(normal_matrix, new_to_old, axis=1)
    arrived = lax.all_to_all(row_slab, ("gx", "gy"), split_axis=1, concat_axis=0, tiled=True)
    column_slab = jnp.take(arrived, new_to_old, axis=0)
    sides_split = lax.all_to_all(right_sides, ("gx", "gy"), split_axis=1, concat_axis=0, tiled=True)
    sides_ordered = jnp.take(sides_split, new_to_old, axis=0)
    renumbered_sides = lax.all_to_all(
        sides_ordered, ("gx", "gy"), split_axis=0, concat_axis=1, tiled=True
    )
    starts = jnp.cumsum(block_lengths) - block_lengths
    block_index = jnp.sum((starts <= self_index).astype(jnp.int32)) - 1
    picked = jnp.arange(starts.shape[0]) == block_index
    first_tile = jnp.sum(jnp.where(picked, starts, 0))
    length = jnp.sum(jnp.where(picked, block_lengths, 0))
    position = self_index - first_tile
    block_span = length - position
    window_tile = jnp.minimum(first_tile, tile_count - MOSTT)
    lead_tiles = self_index - window_tile
    window_rows = MOSTT * tile_width
    window_piece = lax.dynamic_slice_in_dim(column_slab, window_tile * tile_width, window_rows, 0)
    window_pieces = [window_piece] + [
        fetch_columns(window_piece, offset) for offset in range(1, MOSTT)
    ]
    block_matrix = jnp.roll(
        jnp.concatenate(window_pieces, axis=1), -lead_tiles * tile_width, axis=0
    )
    tile_number = jnp.arange(window_rows) // tile_width
    inside = tile_number < block_span
    block_matrix = jnp.where(
        inside[:, None] & inside[None, :], block_matrix, jnp.eye(window_rows, dtype=jnp.float32)
    )
    factor = jnp.linalg.cholesky(block_matrix)

    def precondition(residual):
        gathered = [residual] + [fetch_residual(residual, offset) for offset in range(1, MOSTT)]
        stacked = jnp.where(inside[:, None], jnp.concatenate(gathered, axis=0), 0.0)
        solved = jax.scipy.linalg.cho_solve((factor, True), stacked)
        own_rows = solved[:tile_width]
        for offset in range(1, MOSTT):
            returned = return_solution(
                solved[offset * tile_width : (offset + 1) * tile_width], offset
            )
            own_rows = jnp.where(position == offset, returned, own_rows)
        return own_rows

    iterate = precondition(renumbered_sides)
    iterate = iterate + precondition(
        renumbered_sides
        - (
            jnp.zeros_like(iterate)
            + lax.dot_general(
                column_slab,
                lax.all_gather(iterate, ("gx", "gy"), axis=0, tiled=True),
                (((0,), (0,)), ((), ())),
                precision=lax.Precision.HIGHEST,
                preferred_element_type=jnp.float32,
            )
        )
    )
    return (column_slab, iterate)


def solution(mesh):
    placed = (P(("gx", "gy"), None), P(("gx", "gy"), None), P(), P(), P())
    return jax.shard_map(
        body,
        mesh=mesh,
        in_specs=placed,
        out_specs=(P(None, ("gx", "gy")), P(("gx", "gy"), None)),
        check_vma=False,
    )
```

profile of v0, /device:TPU:2, one launch (start us, length us, event | category | flops | bytes accessed | tf_op | source)
XLA Modules:
  0.0 353.6 jit_solution(17444266172508612999)
XLA Ops:
  0.6 6.1 %all-to-all-start.1 = ((f32[128,32,1]{0,2,1:T(1,128)}), f32[128,32,1]{0,2,1:T(1,128)S(1)}, u32[]{:S(2)}, u32[]{:S(2)}) async-start(f32[128,32,1]{0,2,1:T(1,128)} %bitcast.97), calls=%async_computation.1 | async-start | bytes 32768 | tf_op jit(solution)/shard_map/all_to_all | solution.py:37
  10.2 14.2 %gather_fusion = f32[4096,128]{1,0:T(8,128)} fusion(f32[128,4096]{0,1:T(8,128)S(1)} %copy.19, s32[4096]{0:T(1024)S(1)} %broadcast_clamp_fusion), kind=kCustom, calls=%fused_computation | custom fusion | bytes 4210688 | tf_op jit(solution)/shard_map/jit(_take)/gather | solution.py:34
  24.4 23.0 %gather_fusion.2 = f32[4096]{0:T(1024)S(1)} fusion(f32[4096]{0:T(1024)S(1)} %bitcast.87, s32[4096]{0:T(1024)S(1)} %broadcast_clamp_fusion), kind=kCustom, calls=%fused_computation.2 | custom fusion | bytes 49152 | tf_op jit(solution)/shard_map/jit(_take)/gather | solution.py:38
  48.0 5.8 %all-to-all-start.2 = ((f32[32,128,1]{1,2,0:T(1,128)}), f32[32,128,1]{1,2,0:T(1,128)S(1)}, u32[]{:S(2)}, u32[]{:S(2)}) async-start(f32[32,128,1]{1,2,0:T(1,128)} %bitcast.18), calls=%async_computation.2 | async-start | bytes 32768 | tf_op jit(solution)/shard_map/all_to_all | solution.py:39
  55.6 4.2 %all-to-all-done.2 = f32[32,128,1]{1,2,0:T(1,128)S(1)} async-done(((f32[32,128,1]{1,2,0:T(1,128)}), f32[32,128,1]{1,2,0:T(1,128)S(1)}, u32[]{:S(2)}, u32[]{:S(2)}) %all-to-all-start.2) | async-done | bytes 16416 | tf_op jit(solution)/shard_map/all_to_all | solution.py:39
  59.8 3.8 %all-to-all-start = ((f32[128,32,128]{0,2,1:T(8,128)}), f32[128,32,128]{0,2,1:T(8,128)S(1)}, u32[]{:S(2)}, u32[]{:S(2)}) async-start(f32[128,32,128]{0,2,1:T(8,128)} %broadcast_select_fusion.1), calls=%async_computation | async-start | bytes 4194304 | tf_op jit(solution)/shard_map/all_to_all | solution.py:35
  68.0 6.0 %collective-permute-start.2 = (f32[128,32]{0,1:T(8,128)S(1)}, f32[128,32]{0,1:T(8,128)S(1)}, u32[]{:S(2)}, u32[]{:S(2)}) collective-permute-start(f32[128,32]{0,1:T(8,128)S(1)} %bitcast.92), channel_id=1, source_target_pairs={{1,0},{2,1},{3,2},{4,3},{5,4},{6,5},{7,6},{8,7},{9,8},{10,9},{11,1... | collective-permute-start | bytes 49160 | tf_op jit(solution)/shard_map/ppermute | solution.py:12
  74.0 2.1 collective-permute-start.3
  76.1 36.3 %all-to-all-done = f32[128,32,128]{0,2,1:T(8,128)S(1)} async-done(((f32[128,32,128]{0,2,1:T(8,128)}), f32[128,32,128]{0,2,1:T(8,128)S(1)}, u32[]{:S(2)}, u32[]{:S(2)}) %all-to-all-start) | async-done | bytes 2097184 | tf_op jit(solution)/shard_map/all_to_all | solution.py:35
  115.6 14.2 %gather_fusion.1 = f32[4096,128]{1,0:T(8,128)} fusion(f32[4096,128]{1,0:T(8,128)S(1)} %bitcast.88, s32[4096]{0:T(1024)S(1)} %broadcast_clamp_fusion), kind=kCustom, calls=%fused_computation.1 | custom fusion | bytes 4210688 | tf_op jit(solution)/shard_map/jit(_take)/gather | solution.py:36
  129.8 2.9 copy.21
  134.6 3.7 %collective-permute-start = (f32[384,128]{0,1:T(8,128)S(1)}, f32[384,128]{0,1:T(8,128)S(1)}, u32[]{:S(2)}, u32[]{:S(2)}) collective-permute-start(f32[384,128]{0,1:T(8,128)S(1)} %constant_dynamic-slice_fusion.1), channel_id=1, source_target_pairs={{1,0},{2,1},{3,2},{4,3},{5,4},{6,5},{7,6},{8,7},{9,8},{10,9},{11,1... | collective-permute-start | bytes 589832 | tf_op jit(solution)/shard_map/ppermute | solution.py:12
  138.3 2.4 collective-permute-start.1
  140.7 3.1 collective-permute-done
  143.9 4.3 %collective-permute-done.1 = f32[384,128]{0,1:T(8,128)S(1)} collective-permute-done((f32[384,128]{0,1:T(8,128)S(1)}, f32[384,128]{0,1:T(8,128)S(1)}, u32[]{:S(2)}, u32[]{:S(2)}) %collective-permute-start.1) | collective-permute-done | bytes 196640 | tf_op jit(solution)/shard_map/ppermute | solution.py:12
  150.0 11.7 %cholesky.77 = f32[128,128]{1,0:T(8,128)S(1)} custom-call(f32[128,128]{1,0:T(8,128)S(1)} %cholesky.192), custom_call_target="Cholesky" | custom-call | tf_op jit(solution)/shard_map/jit(cholesky)/cholesky | solution.py:64
  161.8 9.8 %custom-call.24 = f32[1,128,128]{1,2,0:T(8,128)S(1)} custom-call(f32[1,128,128]{2,1,0:T(8,128)S(1)} %get-tuple-element.47), custom_call_target="InvertDiagBlocksLowerTriangular" | custom-call | tf_op jit(solution)/shard_map/jit(cholesky)/cholesky | solution.py:64
  174.0 11.7 %cholesky.162 = f32[128,128]{1,0:T(8,128)S(1)} custom-call(f32[128,128]{1,0:T(8,128)S(1)} %cholesky.196), custom_call_target="Cholesky" | custom-call | tf_op jit(solution)/shard_map/jit(cholesky)/cholesky | solution.py:64
  187.1 10.0 %custom-call.25 = f32[1,128,128]{1,2,0:T(8,128)S(1)} custom-call(f32[1,128,128]{2,1,0:T(8,128)S(1)} %get-tuple-element.44), custom_call_target="InvertDiagBlocksLowerTriangular" | custom-call | tf_op jit(solution)/shard_map/jit(cholesky)/cholesky | solution.py:64
  198.4 11.7 %cholesky.181 = f32[128,128]{1,0:T(8,128)S(1)} custom-call(f32[128,128]{1,0:T(8,128)S(1)} %convolution_subtract_fusion.1), custom_call_target="Cholesky" | custom-call | tf_op jit(solution)/shard_map/jit(cholesky)/cholesky | solution.py:64
  212.8 6.4 %while.4 = (s32[]{:T(128)}, f32[384,384]{1,0:T(8,128)S(1)}, s32[3,2]{0,1:T(2,128)S(1)}, f32[3,128,128]{2,1,0:T(8,128)S(1)}, s32[]{:T(128)}) while((s32[]{:T(128)}, f32[384,384]{1,0:T(8,128)S(1)}, s32[3,2]{0,1:T(2,128)S(1)}, f32[3,128,128]{2,1,0:T(8,128)S(1)}, s32[]{:T(128)}) %tuple.40), condition=%wide.while_cond, body=%wide.while_body.sunk | while | flops 2 | bytes 131181 | solution.py:69
  219.1 29.5 %custom-call.27 = f32[3,128,128]{1,2,0:T(8,128)S(1)} custom-call(f32[3,128,128]{2,1,0:T(8,128)S(1)} %get-tuple-element.17), custom_call_target="InvertDiagBlocksLowerTriangular" | custom-call | tf_op jit(solution)/shard_map/jit(_cho_solve)/triangular_solve | solution.py:69
  250.0 1.9 collective-permute-start.4
  252.2 1.9 collective-permute-start.5
  254.3 6.5 %collective-permute-done.5 = f32[128,32]{0,1:T(8,128)S(1)} collective-permute-done((f32[128,32]{0,1:T(8,128)S(1)}, f32[128,32]{0,1:T(8,128)S(1)}, u32[]{:S(2)}, u32[]{:S(2)}) %collective-permute-start.5) | collective-permute-done | bytes 16416 | tf_op jit(solution)/shard_map/ppermute | solution.py:12
  261.0 66.3 %all_gather.3 = f32[4096,32]{0,1:T(8,128)S(1)} all-gather(f32[128,32]{0,1:T(8,128)S(1)} %fusion.2), channel_id=1, replica_groups=mesh['gx'=4,'gy'=8] {'gx','gy'}, dimensions={0}, use_global_device_ids=true | all-gather | bytes 540672 | tf_op jit(solution)/shard_map/all_gather | solution.py:85
  327.3 2.1 convolution_subtract_fusion.6
  329.4 2.6 collective-permute-start.6
  335.8 2.8 collective-permute-done.7
  339.9 3.9 %collective-permute-start.8 = (f32[128,32]{0,1:T(8,128)S(1)}, f32[128,32]{0,1:T(8,128)S(1)}, u32[]{:S(2)}, u32[]{:S(2)}) collective-permute-start(f32[128,32]{0,1:T(8,128)S(1)} %fusion.29), channel_id=1, source_target_pairs={{0,2},{1,3},{2,4},{3,5},{4,6},{5,7},{6,8},{7,9},{8,10},{9,11},{10,... | collective-permute-start | bytes 49160 | tf_op jit(solution)/shard_map/ppermute | solution.py:12
  344.1 1.9 collective-permute-start.9
  346.2 6.5 %collective-permute-done.9 = f32[128,32]{0,1:T(8,128)S(1)} collective-permute-done((f32[128,32]{0,1:T(8,128)S(1)}, f32[128,32]{0,1:T(8,128)S(1)}, u32[]{:S(2)}, u32[]{:S(2)}) %collective-permute-start.9) | collective-permute-done | bytes 16416 | tf_op jit(solution)/shard_map/ppermute | solution.py:12
  (83 shorter events, 34.6 us)
Async XLA Ops:
  0.6 23.8 %all-to-all-start.1 = ((f32[128,32,1]{0,2,1:T(1,128)}), f32[128,32,1]{0,2,1:T(1,128)S(1)}, u32[]{:S(2)}, u32[]{:S(2)}) async-start(f32[128,32,1]{0,2,1:T(1,128)} %bitcast.97), calls=%async_computation.1 | async-start | bytes 32768 | tf_op jit(solution)/shard_map/all_to_all | solution.py:37
  24.4 29.5 %copy-start.1 = (f32[4096,128]{1,0:T(8,128)S(1)}, f32[4096,128]{1,0:T(8,128)}, u32[]{:S(2)}) copy-start(f32[4096,128]{1,0:T(8,128)} %gather_fusion) | copy-start | bytes 6291460
  48.0 11.7 %all-to-all-start.2 = ((f32[32,128,1]{1,2,0:T(1,128)}), f32[32,128,1]{1,2,0:T(1,128)S(1)}, u32[]{:S(2)}, u32[]{:S(2)}) async-start(f32[32,128,1]{1,2,0:T(1,128)} %bitcast.18), calls=%async_computation.2 | async-start | bytes 32768 | tf_op jit(solution)/shard_map/all_to_all | solution.py:39
  55.6 8.0 %copy-start.3 = (s32[16]{0:T(128)S(1)}, s32[16]{0:T(128)}, u32[]{:S(2)}) copy-start(s32[16]{0:T(128)} %param.11) | copy-start | bytes 196
  59.8 52.6 %all-to-all-start = ((f32[128,32,128]{0,2,1:T(8,128)}), f32[128,32,128]{0,2,1:T(8,128)S(1)}, u32[]{:S(2)}, u32[]{:S(2)}) async-start(f32[128,32,128]{0,2,1:T(8,128)} %broadcast_select_fusion.1), calls=%async_computation | async-start | bytes 4194304 | tf_op jit(solution)/shard_map/all_to_all | solution.py:35
  68.0 72.7 %collective-permute-start.2 = (f32[128,32]{0,1:T(8,128)S(1)}, f32[128,32]{0,1:T(8,128)S(1)}, u32[]{:S(2)}, u32[]{:S(2)}) collective-permute-start(f32[128,32]{0,1:T(8,128)S(1)} %bitcast.92), channel_id=1, source_target_pairs={{1,0},{2,1},{3,2},{4,3},{5,4},{6,5},{7,6},{8,7},{9,8},{10,9},{11,1... | collective-permute-start | bytes 49160 | tf_op jit(solution)/shard_map/ppermute | solution.py:12
  74.0 66.7 %collective-permute-start.3 = (f32[128,32]{0,1:T(8,128)S(1)}, f32[128,32]{0,1:T(8,128)S(1)}, u32[]{:S(2)}, u32[]{:S(2)}) collective-permute-start(f32[128,32]{0,1:T(8,128)S(1)} %bitcast.93), channel_id=1, source_target_pairs={{2,0},{3,1},{4,2},{5,3},{6,4},{7,5},{8,6},{9,7},{10,8},{11,9},{12,... | collective-permute-start | bytes 49160 | tf_op jit(solution)/shard_map/ppermute | solution.py:12
  112.4 1.3 copy-start
  134.6 9.3 %collective-permute-start = (f32[384,128]{0,1:T(8,128)S(1)}, f32[384,128]{0,1:T(8,128)S(1)}, u32[]{:S(2)}, u32[]{:S(2)}) collective-permute-start(f32[384,128]{0,1:T(8,128)S(1)} %constant_dynamic-slice_fusion.1), channel_id=1, source_target_pairs={{1,0},{2,1},{3,2},{4,3},{5,4},{6,5},{7,6},{8,7},{9,8},{10,9},{11,1... | collective-permute-start | bytes 589832 | tf_op jit(solution)/shard_map/ppermute | solution.py:12
  138.3 9.9 %collective-permute-start.1 = (f32[384,128]{0,1:T(8,128)S(1)}, f32[384,128]{0,1:T(8,128)S(1)}, u32[]{:S(2)}, u32[]{:S(2)}) collective-permute-start(f32[384,128]{0,1:T(8,128)S(1)} %constant_dynamic-slice_fusion.1), channel_id=1, source_target_pairs={{2,0},{3,1},{4,2},{5,3},{6,4},{7,5},{8,6},{9,7},{10,8},{11,9},{12,... | collective-permute-start | bytes 589832 | tf_op jit(solution)/shard_map/ppermute | solution.py:12
  149.2 0.8 copy-start.2
  250.0 10.8 %collective-permute-start.4 = (f32[128,32]{0,1:T(8,128)S(1)}, f32[128,32]{0,1:T(8,128)S(1)}, u32[]{:S(2)}, u32[]{:S(2)}) collective-permute-start(f32[128,32]{0,1:T(8,128)S(1)} %fusion.31), channel_id=1, source_target_pairs={{0,2},{1,3},{2,4},{3,5},{4,6},{5,7},{6,8},{7,9},{8,10},{9,11},{10,... | collective-permute-start | bytes 49160 | tf_op jit(solution)/shard_map/ppermute | solution.py:12
  252.2 8.7 %collective-permute-start.5 = (f32[128,32]{0,1:T(8,128)S(1)}, f32[128,32]{0,1:T(8,128)S(1)}, u32[]{:S(2)}, u32[]{:S(2)}) collective-permute-start(f32[128,32]{0,1:T(8,128)S(1)} %fusion.37), channel_id=1, source_target_pairs={{0,1},{1,2},{2,3},{3,4},{4,5},{5,6},{6,7},{7,8},{8,9},{9,10},{10,1... | collective-permute-start | bytes 49160 | tf_op jit(solution)/shard_map/ppermute | solution.py:12
  329.4 6.4 %collective-permute-start.6 = (f32[128,32]{0,1:T(8,128)S(1)}, f32[128,32]{0,1:T(8,128)S(1)}, u32[]{:S(2)}, u32[]{:S(2)}) collective-permute-start(f32[128,32]{0,1:T(8,128)S(1)} %convolution_subtract_fusion.6), channel_id=1, source_target_pairs={{1,0},{2,1},{3,2},{4,3},{5,4},{6,5},{7,6},{8,7},{9,8},{10,9},{11,1... | collective-permute-start | bytes 49160 | tf_op jit(solution)/shard_map/ppermute | solution.py:12
  332.0 6.5 %collective-permute-start.7 = (f32[128,32]{0,1:T(8,128)S(1)}, f32[128,32]{0,1:T(8,128)S(1)}, u32[]{:S(2)}, u32[]{:S(2)}) collective-permute-start(f32[128,32]{0,1:T(8,128)S(1)} %convolution_subtract_fusion.6), channel_id=1, source_target_pairs={{2,0},{3,1},{4,2},{5,3},{6,4},{7,5},{8,6},{9,7},{10,8},{11,9},{12,... | collective-permute-start | bytes 49160 | tf_op jit(solution)/shard_map/ppermute | solution.py:12
  339.9 12.8 %collective-permute-start.8 = (f32[128,32]{0,1:T(8,128)S(1)}, f32[128,32]{0,1:T(8,128)S(1)}, u32[]{:S(2)}, u32[]{:S(2)}) collective-permute-start(f32[128,32]{0,1:T(8,128)S(1)} %fusion.29), channel_id=1, source_target_pairs={{0,2},{1,3},{2,4},{3,5},{4,6},{5,7},{6,8},{7,9},{8,10},{9,11},{10,... | collective-permute-start | bytes 49160 | tf_op jit(solution)/shard_map/ppermute | solution.py:12
  344.1 8.7 %collective-permute-start.9 = (f32[128,32]{0,1:T(8,128)S(1)}, f32[128,32]{0,1:T(8,128)S(1)}, u32[]{:S(2)}, u32[]{:S(2)}) collective-permute-start(f32[128,32]{0,1:T(8,128)S(1)} %fusion.35), channel_id=1, source_target_pairs={{0,1},{1,2},{2,3},{3,4},{4,5},{5,6},{6,7},{7,8},{8,9},{9,10},{10,1... | collective-permute-start | bytes 49160 | tf_op jit(solution)/shard_map/ppermute | solution.py:12
where the time goes:
time: 354 us
  other arithmetic  94.5 us (27%)
  local copies, waits for them, and re-layouts  68.8 us (19%)
  blocking collectives  66.3 us (19%)
  waiting for transfers between devices  63.8 us (18%)
  starting transfers between devices  44.2 us (12%)
  matrix products  10.2 us (3%)
  between operations  5.73 us (2%)
    all_gather x1, blocking collectives, body(): lax.all_gather(iterate, ('gx', 'gy'), axis=0, tiled=True)  66.3 us
    another operation x11, other arithmetic, body(): factor = jnp.linalg.cholesky(block_matrix)  57 us
    all_to_all x1, waiting for transfers between devices, body(): lax.all_to_all(row_slab, ('gx', 'gy'), split_axis=1, concat_axis=0, tiled...  36.3 us
    another operation x4, other arithmetic, precondition(): solved = jax.scipy.linalg.cho_solve((factor, True), stacked)  29.5 us
    ppermute x10, starting transfers between devices, from_behind(): lax.ppermute(value, axis, [(source, source + steps) for source in range(l...  28.5 us
    ppermute x10, waiting for transfers between devices, from_behind(): lax.ppermute(value, axis, [(source, source + steps) for source in range(l...  23.3 us
    gather x1, local copies, waits for them, and re-layouts, body(): sides_ordered = jnp.take(sides_split, new_to_old, axis=0)  23 us
    gather x2, local copies, waits for them, and re-layouts, body(): column_slab = jnp.take(arrived, new_to_old, axis=0)  17.1 us
  transfers between devices with their start and end apart: 13, of which 7 were waited for; matrix products, arithmetic and copies ran while one was open for 13% of the time, Pallas kernels for 0%

commit v1 on v0

--- a/solution.py
+++ b/solution.py
@@ -32,7 +32,12 @@
     self_index = lax.axis_index(("gx", "gy"))
     new_to_old = (tile_order[:, None] * tile_width + inner_order).reshape(-1)
     row_slab = jnp.take(normal_matrix, new_to_old, axis=1)
-    arrived = lax.all_to_all(row_slab, ("gx", "gy"), split_axis=1, concat_axis=0, tiled=True)
+    arrived = jnp.concatenate(
+        lax.all_to_all(
+            jnp.stack(jnp.split(row_slab, lax.axis_size(("gx", "gy")), axis=1)), ("gx", "gy"), 0, 0
+        ),
+        axis=0,
+    )
     column_slab = jnp.take(arrived, new_to_old, axis=0)
     sides_split = lax.all_to_all(right_sides, ("gx", "gy"), split_axis=1, concat_axis=0, tiled=True)
     sides_ordered = jnp.take(sides_split, new_to_old, axis=0)

time: 354 us -> 376 us (1.062)
  local copies, waits for them, and re-layouts: 68.8 us -> 88.9 us
    unnamed x10 -> x37, local copies, waits for them, and re-layouts: 5.86 us -> 24.3 us
    gather x1 -> x2, local copies, waits for them, and re-layouts: 14.2 us -> 17.1 us  [body(): row_slab = jnp.take(normal_matrix, new_to_old, axis=1)]
  transfers between devices with their start and end apart: 13 -> 13, of which waited for: 7 -> 7; matrix products, arithmetic and copies ran while one was open for 13% -> 18% of each run, Pallas kernels for 0% -> 0%
where the time goes in v1:
time: 376 us; the launch traced here: 375 us
  other arithmetic  94.6 us (25%)
  local copies, waits for them, and re-layouts  88.9 us (24%)
  blocking collectives  66.2 us (18%)
  waiting for transfers between devices  64.9 us (17%)
  starting transfers between devices  44.3 us (12%)
  matrix products  10.2 us (3%)
  between operations  5.73 us (2%)
    all_gather x1, blocking collectives, body(): lax.all_gather(iterate, ('gx', 'gy'), axis=0, tiled=True)  66.2 us
    another operation x11, other arithmetic, body(): factor = jnp.linalg.cholesky(block_matrix)  57 us
    all_to_all x1, waiting for transfers between devices, body(): lax.all_to_all(jnp.stack(jnp.split(row_slab, lax.axis_size(('gx', 'gy')),...  36.3 us
    another operation x4, other arithmetic, precondition(): solved = jax.scipy.linalg.cho_solve((factor, True), stacked)  29.5 us
    ppermute x10, starting transfers between devices, from_behind(): lax.ppermute(value, axis, [(source, source + steps) for source in range(l...  28.6 us
    unnamed x37, local copies, waits for them, and re-layouts  24.3 us
    ppermute x10, waiting for transfers between devices, from_behind(): lax.ppermute(value, axis, [(source, source + steps) for source in range(l...  23.3 us
    gather x1, local copies, waits for them, and re-layouts, body(): sides_ordered = jnp.take(sides_split, new_to_old, axis=0)  23 us
  transfers between devices with their start and end apart: 13, of which 7 were waited for; matrix products, arithmetic and copies ran while one was open for 18% of the time, Pallas kernels for 0%

profile of v1, /device:TPU:2, one launch (start us, length us, event | category | flops | bytes accessed | tf_op | source)
XLA Modules:
  0.0 374.8 jit_solution(5585157542012826302)
XLA Ops:
  0.6 6.1 %all-to-all-start.1 = ((f32[128,32,1]{0,2,1:T(1,128)}), f32[128,32,1]{0,2,1:T(1,128)S(1)}, u32[]{:S(2)}, u32[]{:S(2)}) async-start(f32[128,32,1]{0,2,1:T(1,128)} %bitcast.221), calls=%async_computation.1 | async-start | bytes 32768 | tf_op jit(solution)/shard_map/all_to_all | solution.py:42
  10.2 14.2 %gather_fusion = f32[4096,128]{1,0:T(8,128)} fusion(f32[128,4096]{0,1:T(8,128)S(1)} %copy.19, s32[4096]{0:T(1024)S(1)} %broadcast_clamp_fusion), kind=kCustom, calls=%fused_computation | custom fusion | bytes 4210688 | tf_op jit(solution)/shard_map/jit(_take)/gather | solution.py:34
  24.4 2.9 copy.20
  48.9 23.0 %gather_fusion.2 = f32[4096]{0:T(1024)S(1)} fusion(f32[4096]{0:T(1024)S(1)} %bitcast.213, s32[4096]{0:T(1024)S(1)} %broadcast_clamp_fusion), kind=kCustom, calls=%fused_computation.2 | custom fusion | bytes 49152 | tf_op jit(solution)/shard_map/jit(_take)/gather | solution.py:43
  72.5 5.8 %all-to-all-start.2 = ((f32[32,128,1]{1,2,0:T(1,128)}), f32[32,128,1]{1,2,0:T(1,128)S(1)}, u32[]{:S(2)}, u32[]{:S(2)}) async-start(f32[32,128,1]{1,2,0:T(1,128)} %bitcast.48), calls=%async_computation.2 | async-start | bytes 32768 | tf_op jit(solution)/shard_map/all_to_all | solution.py:44
  79.0 5.3 %all-to-all-done.2 = f32[32,128,1]{1,2,0:T(1,128)S(1)} async-done(((f32[32,128,1]{1,2,0:T(1,128)}), f32[32,128,1]{1,2,0:T(1,128)S(1)}, u32[]{:S(2)}, u32[]{:S(2)}) %all-to-all-start.2) | async-done | bytes 16416 | tf_op jit(solution)/shard_map/all_to_all | solution.py:44
  84.3 3.8 %all-to-all-start = ((f32[32,128,128]{2,1,0:T(8,128)}), f32[32,128,128]{2,1,0:T(8,128)S(1)}, u32[]{:S(2)}, u32[]{:S(2)}) async-start(f32[32,128,128]{2,1,0:T(8,128)} %fusion.21), calls=%async_computation | async-start | bytes 4194304 | tf_op jit(solution)/shard_map/all_to_all | solution.py:36
  92.5 6.0 %collective-permute-start.2 = (f32[128,32]{0,1:T(8,128)S(1)}, f32[128,32]{0,1:T(8,128)S(1)}, u32[]{:S(2)}, u32[]{:S(2)}) collective-permute-start(f32[128,32]{0,1:T(8,128)S(1)} %bitcast.216), channel_id=1, source_target_pairs={{1,0},{2,1},{3,2},{4,3},{5,4},{6,5},{7,6},{8,7},{9,8},{10,9},{11,1... | collective-permute-start | bytes 49160 | tf_op jit(solution)/shard_map/ppermute | solution.py:12
  98.5 2.1 collective-permute-start.3
  100.6 36.3 %all-to-all-done = f32[32,128,128]{2,1,0:T(8,128)S(1)} async-done(((f32[32,128,128]{2,1,0:T(8,128)}), f32[32,128,128]{2,1,0:T(8,128)S(1)}, u32[]{:S(2)}, u32[]{:S(2)}) %all-to-all-start) | async-done | bytes 2097184 | tf_op jit(solution)/shard_map/all_to_all | solution.py:36
  136.9 14.2 %gather_fusion.1 = f32[4096,128]{1,0:T(8,128)} fusion(f32[4096,128]{1,0:T(8,128)S(1)} %bitcast.214, s32[4096]{0:T(1024)S(1)} %broadcast_clamp_fusion), kind=kCustom, calls=%fused_computation.1 | custom fusion | bytes 4210688 | tf_op jit(solution)/shard_map/jit(_take)/gather | solution.py:41
  151.1 2.9 copy.21
  155.8 3.7 collective-permute-start
  159.5 2.4 collective-permute-start.1
  162.0 3.1 collective-permute-done
  165.1 4.3 %collective-permute-done.1 = f32[384,128]{0,1:T(8,128)S(1)} collective-permute-done((f32[384,128]{0,1:T(8,128)S(1)}, f32[384,128]{0,1:T(8,128)S(1)}, u32[]{:S(2)}, u32[]{:S(2)}) %collective-permute-start.1) | collective-permute-done | bytes 196640 | tf_op jit(solution)/shard_map/ppermute | solution.py:12
  171.3 11.7 %cholesky.77 = f32[128,128]{1,0:T(8,128)S(1)} custom-call(f32[128,128]{1,0:T(8,128)S(1)} %cholesky.192), custom_call_target="Cholesky" | custom-call | tf_op jit(solution)/shard_map/jit(cholesky)/cholesky | solution.py:69
  183.1 9.8 %custom-call.24 = f32[1,128,128]{1,2,0:T(8,128)S(1)} custom-call(f32[1,128,128]{2,1,0:T(8,128)S(1)} %get-tuple-element.45), custom_call_target="InvertDiagBlocksLowerTriangular" | custom-call | tf_op jit(solution)/shard_map/jit(cholesky)/cholesky | solution.py:69
  195.3 11.7 %cholesky.162 = f32[128,128]{1,0:T(8,128)S(1)} custom-call(f32[128,128]{1,0:T(8,128)S(1)} %cholesky.196), custom_call_target="Cholesky" | custom-call | tf_op jit(solution)/shard_map/jit(cholesky)/cholesky | solution.py:69
  208.4 10.0 %custom-call.25 = f32[1,128,128]{1,2,0:T(8,128)S(1)} custom-call(f32[1,128,128]{2,1,0:T(8,128)S(1)} %get-tuple-element.42), custom_call_target="InvertDiagBlocksLowerTriangular" | custom-call | tf_op jit(solution)/shard_map/jit(cholesky)/cholesky | solution.py:69
  219.7 11.7 %cholesky.181 = f32[128,128]{1,0:T(8,128)S(1)} custom-call(f32[128,128]{1,0:T(8,128)S(1)} %convolution_subtract_fusion.1), custom_call_target="Cholesky" | custom-call | tf_op jit(solution)/shard_map/jit(cholesky)/cholesky | solution.py:69
  234.0 6.4 %while.4 = (s32[]{:T(128)}, f32[384,384]{1,0:T(8,128)S(1)}, s32[3,2]{0,1:T(2,128)S(1)}, f32[3,128,128]{2,1,0:T(8,128)S(1)}, s32[]{:T(128)}) while((s32[]{:T(128)}, f32[384,384]{1,0:T(8,128)S(1)}, s32[3,2]{0,1:T(2,128)S(1)}, f32[3,128,128]{2,1,0:T(8,128)S(1)}, s32[]{:T(128)}) %tuple.39), condition=%wide.while_cond, body=%wide.while_body.sunk | while | flops 2 | bytes 131181 | solution.py:74
  240.4 29.5 %custom-call.27 = f32[3,128,128]{1,2,0:T(8,128)S(1)} custom-call(f32[3,128,128]{2,1,0:T(8,128)S(1)} %get-tuple-element.17), custom_call_target="InvertDiagBlocksLowerTriangular" | custom-call | tf_op jit(solution)/shard_map/jit(_cho_solve)/triangular_solve | solution.py:74
  273.4 1.9 collective-permute-start.5
  275.6 6.5 %collective-permute-done.5 = f32[128,32]{0,1:T(8,128)S(1)} collective-permute-done((f32[128,32]{0,1:T(8,128)S(1)}, f32[128,32]{0,1:T(8,128)S(1)}, u32[]{:S(2)}, u32[]{:S(2)}) %collective-permute-start.5) | collective-permute-done | bytes 16416 | tf_op jit(solution)/shard_map/ppermute | solution.py:12
  282.3 66.2 %all_gather.3 = f32[4096,32]{0,1:T(8,128)S(1)} all-gather(f32[128,32]{0,1:T(8,128)S(1)} %fusion.2), channel_id=1, replica_groups=mesh['gx'=4,'gy'=8] {'gx','gy'}, dimensions={0}, use_global_device_ids=true | all-gather | bytes 540672 | tf_op jit(solution)/shard_map/all_gather | solution.py:90
  348.5 2.1 convolution_subtract_fusion.6
  350.5 2.7 collective-permute-start.6
  357.0 2.8 collective-permute-done.7
  361.2 3.9 %collective-permute-start.8 = (f32[128,32]{0,1:T(8,128)S(1)}, f32[128,32]{0,1:T(8,128)S(1)}, u32[]{:S(2)}, u32[]{:S(2)}) collective-permute-start(f32[128,32]{0,1:T(8,128)S(1)} %fusion.61), channel_id=1, source_target_pairs={{0,2},{1,3},{2,4},{3,5},{4,6},{5,7},{6,8},{7,9},{8,10},{9,11},{10,... | collective-permute-start | bytes 49160 | tf_op jit(solution)/shard_map/ppermute | solution.py:12
  365.3 1.9 collective-permute-start.9
  367.5 6.5 %collective-permute-done.9 = f32[128,32]{0,1:T(8,128)S(1)} collective-permute-done((f32[128,32]{0,1:T(8,128)S(1)}, f32[128,32]{0,1:T(8,128)S(1)}, u32[]{:S(2)}, u32[]{:S(2)}) %collective-permute-start.9) | collective-permute-done | bytes 16416 | tf_op jit(solution)/shard_map/ppermute | solution.py:12
  (111 shorter events, 53.8 us)
Async XLA Ops:
  0.6 48.3 %all-to-all-start.1 = ((f32[128,32,1]{0,2,1:T(1,128)}), f32[128,32,1]{0,2,1:T(1,128)S(1)}, u32[]{:S(2)}, u32[]{:S(2)}) async-start(f32[128,32,1]{0,2,1:T(1,128)} %bitcast.221), calls=%async_computation.1 | async-start | bytes 32768 | tf_op jit(solution)/shard_map/all_to_all | solution.py:42
  72.5 11.7 %all-to-all-start.2 = ((f32[32,128,1]{1,2,0:T(1,128)}), f32[32,128,1]{1,2,0:T(1,128)S(1)}, u32[]{:S(2)}, u32[]{:S(2)}) async-start(f32[32,128,1]{1,2,0:T(1,128)} %bitcast.48), calls=%async_computation.2 | async-start | bytes 32768 | tf_op jit(solution)/shard_map/all_to_all | solution.py:44
  79.0 9.0 %copy-start.1 = (s32[16]{0:T(128)S(1)}, s32[16]{0:T(128)}, u32[]{:S(2)}) copy-start(s32[16]{0:T(128)} %param.11) | copy-start | bytes 196
  84.3 52.6 %all-to-all-start = ((f32[32,128,128]{2,1,0:T(8,128)}), f32[32,128,128]{2,1,0:T(8,128)S(1)}, u32[]{:S(2)}, u32[]{:S(2)}) async-start(f32[32,128,128]{2,1,0:T(8,128)} %fusion.21), calls=%async_computation | async-start | bytes 4194304 | tf_op jit(solution)/shard_map/all_to_all | solution.py:36
  92.5 69.5 %collective-permute-start.2 = (f32[128,32]{0,1:T(8,128)S(1)}, f32[128,32]{0,1:T(8,128)S(1)}, u32[]{:S(2)}, u32[]{:S(2)}) collective-permute-start(f32[128,32]{0,1:T(8,128)S(1)} %bitcast.216), channel_id=1, source_target_pairs={{1,0},{2,1},{3,2},{4,3},{5,4},{6,5},{7,6},{8,7},{9,8},{10,9},{11,1... | collective-permute-start | bytes 49160 | tf_op jit(solution)/shard_map/ppermute | solution.py:12
  98.5 63.4 %collective-permute-start.3 = (f32[128,32]{0,1:T(8,128)S(1)}, f32[128,32]{0,1:T(8,128)S(1)}, u32[]{:S(2)}, u32[]{:S(2)}) collective-permute-start(f32[128,32]{0,1:T(8,128)S(1)} %bitcast.217), channel_id=1, source_target_pairs={{2,0},{3,1},{4,2},{5,3},{6,4},{7,5},{8,6},{9,7},{10,8},{11,9},{12,... | collective-permute-start | bytes 49160 | tf_op jit(solution)/shard_map/ppermute | solution.py:12
  155.8 9.3 %collective-permute-start = (f32[384,128]{0,1:T(8,128)S(1)}, f32[384,128]{0,1:T(8,128)S(1)}, u32[]{:S(2)}, u32[]{:S(2)}) collective-permute-start(f32[384,128]{0,1:T(8,128)S(1)} %constant_dynamic-slice_fusion.1), channel_id=1, source_target_pairs={{1,0},{2,1},{3,2},{4,3},{5,4},{6,5},{7,6},{8,7},{9,8},{10,9},{11,1... | collective-permute-start | bytes 589832 | tf_op jit(solution)/shard_map/ppermute | solution.py:12
  159.5 9.9 %collective-permute-start.1 = (f32[384,128]{0,1:T(8,128)S(1)}, f32[384,128]{0,1:T(8,128)S(1)}, u32[]{:S(2)}, u32[]{:S(2)}) collective-permute-start(f32[384,128]{0,1:T(8,128)S(1)} %constant_dynamic-slice_fusion.1), channel_id=1, source_target_pairs={{2,0},{3,1},{4,2},{5,3},{6,4},{7,5},{8,6},{9,7},{10,8},{11,9},{12,... | collective-permute-start | bytes 589832 | tf_op jit(solution)/shard_map/ppermute | solution.py:12
  170.5 0.8 copy-start
  271.3 10.8 %collective-permute-start.4 = (f32[128,32]{0,1:T(8,128)S(1)}, f32[128,32]{0,1:T(8,128)S(1)}, u32[]{:S(2)}, u32[]{:S(2)}) collective-permute-start(f32[128,32]{0,1:T(8,128)S(1)} %fusion.63), channel_id=1, source_target_pairs={{0,2},{1,3},{2,4},{3,5},{4,6},{5,7},{6,8},{7,9},{8,10},{9,11},{10,... | collective-permute-start | bytes 49160 | tf_op jit(solution)/shard_map/ppermute | solution.py:12
  273.4 8.7 %collective-permute-start.5 = (f32[128,32]{0,1:T(8,128)S(1)}, f32[128,32]{0,1:T(8,128)S(1)}, u32[]{:S(2)}, u32[]{:S(2)}) collective-permute-start(f32[128,32]{0,1:T(8,128)S(1)} %fusion.69), channel_id=1, source_target_pairs={{0,1},{1,2},{2,3},{3,4},{4,5},{5,6},{6,7},{7,8},{8,9},{9,10},{10,1... | collective-permute-start | bytes 49160 | tf_op jit(solution)/shard_map/ppermute | solution.py:12
  350.5 6.5 %collective-permute-start.6 = (f32[128,32]{0,1:T(8,128)S(1)}, f32[128,32]{0,1:T(8,128)S(1)}, u32[]{:S(2)}, u32[]{:S(2)}) collective-permute-start(f32[128,32]{0,1:T(8,128)S(1)} %convolution_subtract_fusion.6), channel_id=1, source_target_pairs={{1,0},{2,1},{3,2},{4,3},{5,4},{6,5},{7,6},{8,7},{9,8},{10,9},{11,1... | collective-permute-start | bytes 49160 | tf_op jit(solution)/shard_map/ppermute | solution.py:12
  353.3 6.5 %collective-permute-start.7 = (f32[128,32]{0,1:T(8,128)S(1)}, f32[128,32]{0,1:T(8,128)S(1)}, u32[]{:S(2)}, u32[]{:S(2)}) collective-permute-start(f32[128,32]{0,1:T(8,128)S(1)} %convolution_subtract_fusion.6), channel_id=1, source_target_pairs={{2,0},{3,1},{4,2},{5,3},{6,4},{7,5},{8,6},{9,7},{10,8},{11,9},{12,... | collective-permute-start | bytes 49160 | tf_op jit(solution)/shard_map/ppermute | solution.py:12
  361.2 12.8 %collective-permute-start.8 = (f32[128,32]{0,1:T(8,128)S(1)}, f32[128,32]{0,1:T(8,128)S(1)}, u32[]{:S(2)}, u32[]{:S(2)}) collective-permute-start(f32[128,32]{0,1:T(8,128)S(1)} %fusion.61), channel_id=1, source_target_pairs={{0,2},{1,3},{2,4},{3,5},{4,6},{5,7},{6,8},{7,9},{8,10},{9,11},{10,... | collective-permute-start | bytes 49160 | tf_op jit(solution)/shard_map/ppermute | solution.py:12
  365.3 8.7 %collective-permute-start.9 = (f32[128,32]{0,1:T(8,128)S(1)}, f32[128,32]{0,1:T(8,128)S(1)}, u32[]{:S(2)}, u32[]{:S(2)}) collective-permute-start(f32[128,32]{0,1:T(8,128)S(1)} %fusion.67), channel_id=1, source_target_pairs={{0,1},{1,2},{2,3},{3,4},{4,5},{5,6},{6,7},{7,8},{8,9},{9,10},{10,1... | collective-permute-start | bytes 49160 | tf_op jit(solution)/shard_map/ppermute | solution.py:12
